TPU v7x, 256 devices: a whole 4x4x8 slice. The times are simulated.
256 devices in a mesh: t: 4 (over x), v: 64 (over z, y, core).
Axes of the slice: x: 4, y: 4, z: 8, core: 2. Of those that a mesh axis runs over, the one named last changes fastest.
Arguments:
- hidden_in: bfloat16 [256, 2304], replicated
- seq_lens: int32 [256], replicated
- target: int32 [256], replicated
- g_attn_pre: bfloat16 [2304], replicated
- w_q: bfloat16 [2304, 2048], P(None, 't')
- w_k: bfloat16 [2304, 1024], P(None, 't')
- w_v: bfloat16 [2304, 1024], P(None, 't')
- w_o: bfloat16 [2048, 2304], P('t')
- g_attn_post: bfloat16 [2304], replicated
- g_mlp_pre: bfloat16 [2304], replicated
- w_gate: bfloat16 [2304, 9216], P(None, 't')
- w_up: bfloat16 [2304, 9216], P(None, 't')
- w_down: bfloat16 [9216, 2304], P('t')
- g_mlp_post: bfloat16 [2304], replicated
- g_final: bfloat16 [2304], replicated
- k_cache: bfloat16 [256, 256, 4, 256], P(None, None, 't')
- v_cache: bfloat16 [256, 256, 4, 256], P(None, None, 't')
- embed_table: bfloat16 [256000, 2304], P(('v', 't'))
Outputs:
- output 1: float32 [256], replicated
- output 2: bfloat16 [256, 2304], replicated
All inputs are finite; a program needn't handle non-finite values.
Results may differ from a plain program's by a relative error of at most 0.00723531.
Values sent between devices are 32-bit elements.
A program may use at most 768 MiB of HBM per device.

v0:
```python
import jax
import jax.numpy as jnp
from jax import lax
from jax.sharding import PartitionSpec as P

ATTN_CAP = 50.0
FINAL_CAP = 30.0
NORM_EPS = 1e-6
ROPE_BASE = 10000.0


def rms_norm(values, gain_vec):
    x_f32 = values.astype(jnp.float32)
    scaled = x_f32 * lax.rsqrt(jnp.mean(x_f32 * x_f32, axis=-1, keepdims=True) + NORM_EPS)
    return scaled * (1.0 + gain_vec.astype(jnp.float32))


def rotary(values, positions):
    half_dim = values.shape[-1] // 2
    inv_freq = ROPE_BASE ** (-2.0 * jnp.arange(half_dim, dtype=jnp.float32) / values.shape[-1])
    angles = positions.astype(jnp.float32)[:, None] * inv_freq[None, :]
    angles = angles.reshape((values.shape[0],) + (1,) * (values.ndim - 2) + (half_dim,))
    cos_t = jnp.cos(angles)
    sin_t = jnp.sin(angles)
    x_low = values[..., :half_dim]
    x_high = values[..., half_dim:]
    return jnp.concatenate([x_low * cos_t - x_high * sin_t, x_high * cos_t + x_low * sin_t], axis=-1)


def attention(normed, seq_lens, w_q, w_k, w_v, k_cache, v_cache):
    tokens, ctx_len, kv_heads, head_dim = k_cache.shape
    group_size = w_q.shape[1] // (kv_heads * head_dim)
    score_scale = head_dim ** -0.5
    q_rot = rotary(jnp.dot(normed, w_q, preferred_element_type=jnp.float32).reshape(tokens, kv_heads, group_size, head_dim), seq_lens).astype(jnp.bfloat16)
    k_rot = rotary(jnp.dot(normed, w_k, preferred_element_type=jnp.float32).reshape(tokens, kv_heads, head_dim), seq_lens).astype(jnp.bfloat16)
    v_new = jnp.dot(normed, w_v, preferred_element_type=jnp.float32).astype(jnp.bfloat16).reshape(tokens, kv_heads, head_dim)
    s_cache = jnp.einsum('nkgd,ntkd->nkgt', q_rot, k_cache, preferred_element_type=jnp.float32) * score_scale
    s_new = jnp.einsum('nkgd,nkd->nkg', q_rot, k_rot, preferred_element_type=jnp.float32) * score_scale
    s_cache = ATTN_CAP * jnp.tanh(s_cache / ATTN_CAP)
    s_new = ATTN_CAP * jnp.tanh(s_new / ATTN_CAP)
    valid_mask = jnp.arange(ctx_len)[None, :] < seq_lens[:, None]
    s_cache = jnp.where(valid_mask[:, None, None, :], s_cache, -1e30)
    row_max = jnp.maximum(jnp.max(s_cache, axis=-1), s_new)
    p_cache = jnp.exp(s_cache - row_max[..., None])
    p_new = jnp.exp(s_new - row_max)
    denominator = jnp.sum(p_cache, axis=-1) + p_new
    weighted = jnp.einsum('nkgt,ntkd->nkgd', p_cache.astype(jnp.bfloat16), v_cache, preferred_element_type=jnp.float32)
    weighted = weighted + p_new.astype(jnp.bfloat16).astype(jnp.float32)[..., None] * v_new.astype(jnp.float32)[:, :, None, :]
    return (weighted / denominator[..., None]).astype(jnp.bfloat16).reshape(tokens, kv_heads * group_size * head_dim)


def solution(mesh):
    tp_size = mesh.shape['t']
    in_specs = (P(), P(), P(), P(), P(None, 't'), P(None, 't'), P(None, 't'), P('t', None), P(), P(), P(None, 't'), P(None, 't'), P('t', None), P(), P(), P(None, None, 't', None), P(None, None, 't', None), P(('v', 't'), None))

    def local_step(hidden_in, seq_lens, target, g_attn_pre, w_q, w_k, w_v, w_o, g_attn_post, g_mlp_pre, w_gate, w_up, w_down, g_mlp_post, g_final, k_cache, v_cache, embed_table):
        normed = rms_norm(hidden_in, g_attn_pre).astype(jnp.bfloat16)
        attn_vec = attention(normed, seq_lens, w_q, w_k, w_v, k_cache, v_cache)
        attn_part = jnp.dot(attn_vec, w_o, preferred_element_type=jnp.float32)
        attn_out = lax.psum(attn_part, 't')
        hidden_mid = (hidden_in.astype(jnp.float32) + rms_norm(attn_out, g_attn_post)).astype(jnp.bfloat16)
        mlp_in = rms_norm(hidden_mid, g_mlp_pre).astype(jnp.bfloat16)
        gate_proj = jnp.dot(mlp_in, w_gate, preferred_element_type=jnp.float32)
        up_proj = jnp.dot(mlp_in, w_up, preferred_element_type=jnp.float32)
        activated = (jax.nn.gelu(gate_proj, approximate=True) * up_proj).astype(jnp.bfloat16)
        mlp_part = jnp.dot(activated, w_down, preferred_element_type=jnp.float32)
        mlp_out = lax.psum(mlp_part, 't')
        hidden_out = (hidden_mid.astype(jnp.float32) + rms_norm(mlp_out, g_mlp_post)).astype(jnp.bfloat16)
        final_h = rms_norm(hidden_out, g_final).astype(jnp.bfloat16)
        logits = lax.dot_general(final_h, embed_table, (((1,), (1,)), ((), ())), preferred_element_type=jnp.float32)
        capped = FINAL_CAP * jnp.tanh(logits / FINAL_CAP)
        vocab_local = embed_table.shape[0]
        shard_index = lax.axis_index('v') * tp_size + lax.axis_index('t')
        row_ids = shard_index * vocab_local + jnp.arange(vocab_local)
        local_max = jnp.max(capped, axis=1)
        local_sum = jnp.sum(jnp.exp(capped - local_max[:, None]), axis=1)
        local_tgt = jnp.sum(jnp.where(row_ids[None, :] == target[:, None], capped, 0.0), axis=1)
        gathered = lax.all_gather(jnp.stack([local_max, local_sum, local_tgt]), ('v', 't'))
        glob_max = jnp.max(gathered[:, 0], axis=0)
        glob_sum = jnp.sum(gathered[:, 1] * jnp.exp(gathered[:, 0] - glob_max[None, :]), axis=0)
        logprob = jnp.sum(gathered[:, 2], axis=0) - glob_max - jnp.log(glob_sum)
        return logprob, hidden_out

    return jax.shard_map(local_step, mesh=mesh, in_specs=in_specs, out_specs=(P(), P()), check_vma=False)
```

profile of v0, /device:TPU:1, one launch (start us, length us, event | category | flops | bytes accessed | tf_op | source)
XLA Modules:
  0.0 331.0 jit_solution(16472305820442472296)
XLA Ops:
  8.1 1.4 iota_compare_fusion
  10.2 1.6 fusion.8
  11.8 1.2 multiply_cosine_fusion.1
  13.0 2.4 convolution_bitcast_fusion
  16.8 1.8 copy.39
  18.6 3.3 fusion.82
  21.9 2.2 reshape.310
  24.0 1.4 fusion.70
  26.1 2.0 multiply_reduce_fusion.2
  29.1 16.3 %fusion.86 = (f32[256,2]{1,0:T(8,128)}, f32[256,2,256]{2,1,0:T(2,128)}) fusion(bf16[256,256,1,256]{3,1,2,0:T(8,128)(2,1)} %param.33, bf16[256,2,128]{2,1,0:T(2,128)(2,1)} %copy-done.6, bf16[256,2,128]{2,1,0:T(2,128)(2,1)} %copy-done.5, pred[256,256]{1,0:T(8,128)(4,1)} %iota_compare_fusion), kind=kOutput, calls=%fused_computation.111 | convolution fusion | flops 68156928 | bytes 34408448 | tf_op jit(solution)/shard_map/nkgd,ntkd->nkgt/dot_general | solution.py:37
  47.2 2.4 fusion.55
  51.2 1.5 copy.28
  53.4 2.5 fusion.28
  56.0 16.2 %fusion.41 = bf16[256,2,256]{2,1,0:T(2,128)(2,1)} fusion(bf16[256,256,1,256]{3,1,2,0:T(8,128)(2,1)} %param.34, f32[256,2,256]{2,1,0:T(2,128)} %get-tuple-element.21, f32[256,2]{1,0:T(8,128)} %copy.30, f32[256,256]{1,0:T(8,128)} %fusion.28, f32[256,2]{1,0:T(8,128)} %copy.28, f32[256,2]{1,0:T(8,128)} %copy.27), kind=kOutput, calls=%fused_computation.47 | convolution fusion | flops 67895296 | bytes 34609152 | tf_op jit(solution)/shard_map/nkgt,ntkd->nkgd/dot_general | solution.py:47
  72.1 1.0 copy.40
  73.1 2.2 fusion.88
  76.0 70.8 %all-reduce.3.cloned.1.call-done = f32[256,2304]{1,0:T(8,128)} async-done(((f32[256,2304]{1,0:T(8,128)}), f32[256,2304]{1,0:T(8,128)}) %all-reduce.3.cloned.1.call-update) | async-done | bytes 2359312 | tf_op jit(solution)/shard_map/psum | solution.py:60
  146.9 2.1 multiply_reduce_fusion.1
  149.9 8.4 %fusion.53 = f32[256,2304]{1,0:T(8,128)} fusion(bf16[2304,2304]{1,0:T(8,128)(2,1)} %param.28, bf16[256,2304]{1,0:T(8,128)(2,1)S(1)} %get-tuple-element.9, f32[2304]{0:T(1024)S(1)} %convert_add_fusion.4, f32[256]{0:T(256)S(1)} %add_rsqrt_fusion.2), kind=kOutput, calls=%fused_computation.55 | convolution fusion | flops 2720268288 | bytes 14166016 | tf_op jit(solution)/shard_map/dot_general | solution.py:63
  158.3 15.0 %fusion.50 = f32[256,2304]{1,0:T(8,128)} fusion(bf16[2304,2304]{1,0:T(8,128)(2,1)} %param.30, bf16[2304,2304]{1,0:T(8,128)(2,1)} %param.29, f32[256,2304]{1,0:T(8,128)} %fusion.53, bf16[256,2304]{1,0:T(8,128)(2,1)S(1)} %get-tuple-element.9, f32[2304]{0:T(1024)S(1)} %convert_add_fusion.4, f32[256]{0:T(256)S(1)} %add_rsqrt_fusion.2), kind=kOutput, calls=%fused_computation.52 | convolution fusion | flops 5444075520 | bytes 27142144 | tf_op jit(solution)/shard_map/dot_general | solution.py:66
  174.0 67.2 %all-reduce.5.cloned.1.call-done = f32[256,2304]{1,0:T(8,128)} async-done(((f32[256,2304]{1,0:T(8,128)}), f32[256,2304]{1,0:T(8,128)}) %all-reduce.5.cloned.1.call-update) | async-done | bytes 2359312 | tf_op jit(solution)/shard_map/psum | solution.py:67
  241.2 2.1 multiply_reduce_fusion
  244.3 4.3 %fusion.87 = (f32[256]{0:T(256)S(1)}, f32[256,1000]{0,1:T(8,128)S(1)}) fusion(bf16[1000,2304]{1,0:T(8,128)(2,1)} %param.35, bf16[256,2304]{1,0:T(8,128)(2,1)S(1)} %get-tuple-element.7, f32[2304]{0:T(1024)S(1)} %convert_add_fusion.2, f32[256]{0:T(256)S(1)} %add_rsqrt_fusion), kind=kOutput, calls=%fused_computation.112 | convolution fusion | flops 1182775040 | bytes 6822912 | tf_op jit(solution)/shard_map/dot_general | solution.py:70
  248.9 74.0 %all-gather.1 = f32[256,3,256]{2,1,0:T(4,128)S(1)} all-gather(f32[1,3,256]{2,1,0:T(4,128)S(1)} %maximum_bitcast_fusion), channel_id=2, replica_groups=mesh['t'=4,'v'=64] {'v','t'}, dimensions={0}, use_global_device_ids=true | all-gather | bytes 789504 | tf_op jit(solution)/shard_map/all_gather | solution.py:78
  (63 shorter events, 13.7 us)
Async XLA Ops:
  7.2 66.0 %copy-start = (bf16[512,2304]{1,0:T(8,128)(2,1)S(1)}, bf16[512,2304]{1,0:T(8,128)(2,1)}, u32[]{:S(2)}) copy-start(bf16[512,2304]{1,0:T(8,128)(2,1)} %param.25) | copy-start | bytes 7077892
  7.2 139.7 %all-reduce.3.cloned.1.call-start = ((), (), s32[]{:S(2)}) async-start(), calls=%async_computation | async-start | bytes 4718592 | tf_op jit(solution)/shard_map/psum | solution.py:60
  10.2 8.4 %copy-start.8 = (f32[2304]{0:T(1024)}, f32[2304]{0:T(1024)S(1)}, u32[]{:S(2)}) copy-start(f32[2304]{0:T(1024)S(1)} %convert_add_fusion.6) | copy-start | bytes 27652
  11.8 6.8 %copy-start.13 = (f32[256]{0:T(256)}, f32[256]{0:T(256)S(1)}, u32[]{:S(2)}) copy-start(f32[256]{0:T(256)S(1)} %add_rsqrt_fusion.4) | copy-start | bytes 3076
  13.0 5.5 %copy-start.4 = (bf16[256,2304]{1,0:T(8,128)(2,1)S(1)}, bf16[256,2304]{1,0:T(8,128)(2,1)}, u32[]{:S(2)}) copy-start(bf16[256,2304]{1,0:T(8,128)(2,1)} %param.18) | copy-start | bytes 3538948
  25.4 0.7 copy-start.5
  25.4 0.7 copy-start.6
  75.3 0.7 copy-start.9
  75.3 0.7 copy-start.10
  75.3 165.8 %all-reduce.5.cloned.1.call-start = ((), (), s32[]{:S(2)}) async-start(), calls=%async_computation.1 | async-start | bytes 4718592 | tf_op jit(solution)/shard_map/psum | solution.py:67
  146.9 2.4 copy-start.3
  173.3 0.7 copy-start.11
  173.3 0.7 copy-start.12
  241.2 2.4 copy-start.2
  244.2 4.4 %copy-start.7 = (bf16[256,2304]{1,0:T(8,128)(2,1)}, bf16[256,2304]{1,0:T(8,128)(2,1)S(1)}, u32[]{:S(2)}) copy-start(bf16[256,2304]{1,0:T(8,128)(2,1)S(1)} %get-tuple-element.7) | copy-start | bytes 3538948
  244.2 4.3 %copy-start.14 = (s32[256]{0:T(256)S(1)}, s32[256]{0:T(256)}, u32[]{:S(2)}) copy-start(s32[256]{0:T(256)} %param.20) | copy-start | bytes 3076
  244.2 79.9 %copy-start.1 = (bf16[512,2304]{1,0:T(8,128)(2,1)S(1)}, bf16[512,2304]{1,0:T(8,128)(2,1)}, u32[]{:S(2)}) copy-start(bf16[512,2304]{1,0:T(8,128)(2,1)} %param.25) | copy-start | bytes 7077892
Sparse Core Ops, SparseCore 0:
  75.5 71.3 all-reduce.2
  173.4 67.6 all-reduce.4
where the time goes:
time: 332 us; the launch traced here: 331 us
  waiting for transfers between devices  138 us (42%)
  blocking collectives  74 us (22%)
  matrix products  70.6 us (21%)
  other arithmetic  20.5 us (6%)
  between operations  14.2 us (4%)
  local copies, waits for them, and re-layouts  13.3 us (4%)
    all_gather x1, blocking collectives, local_step(): lax.all_gather(jnp.stack([local_max, local_sum, local_tgt]), ('v', 't'))  74 us
    psum x1, waiting for transfers between devices, local_step(): attn_out = lax.psum(attn_part, 't')  70.8 us
    psum x1, waiting for transfers between devices, local_step(): mlp_out = lax.psum(mlp_part, 't')  67.2 us
    dot_general x1, matrix products, attention(): jnp.einsum('nkgd,ntkd->nkgt', q_rot, k_cache, preferred_element_type=jnp....  16.3 us
    dot_general x1, matrix products, attention(): jnp.einsum('nkgt,ntkd->nkgd', p_cache.astype(jnp.bfloat16), v_cache, pref...  16.2 us
    dot_general x1, matrix products, local_step(): mlp_part = jnp.dot(activated, w_down, preferred_element_type=jnp.float32)  15 us
    dot_general x1, matrix products, local_step(): gate_proj = jnp.dot(mlp_in, w_gate, preferred_element_type=jnp.float32)  8.38 us
    reduce_sum x5, other arithmetic, rms_norm(): jnp.mean(x_f32 * x_f32, axis=-1, keepdims=True) + NORM_EPS  7.02 us
  transfers between devices with their start and end apart: 2, of which 2 were waited for; matrix products, arithmetic and copies ran while one was open for 0% of the time, Pallas kernels for 0%

commit v1 on v0

v1 whole, which is shorter than its diff:
```python
import functools

import jax
import jax.numpy as jnp
import numpy as np
from jax import lax
from jax.experimental import pallas as pl
from jax.experimental.pallas import tpu as pltpu
from jax.sharding import PartitionSpec as P

ATTN_CAP = 50.0
FINAL_CAP = 30.0
NORM_EPS = 1e-6
ROPE_BASE = 10000.0
MESH = pl.DeviceIdType.MESH
F32 = jnp.float32
BF16 = jnp.bfloat16


def dot(a, b):
    return jnp.dot(a, b, preferred_element_type=F32)


def dot_nt(a, b):
    return lax.dot_general(a, b, (((1,), (1,)), ((), ())), preferred_element_type=F32)


def rms(values, gain):
    mean_sq = jnp.mean(values * values, axis=-1, keepdims=True)
    return values * lax.rsqrt(mean_sq + NORM_EPS) * (1.0 + gain)


def kernel(NT, NY, NZ, seq, hid, tgt, inv_freq, g_ap, g_ao, g_mp, g_mo, g_fi, wq, wk, wv, wo, wg, wu, wd, kc, vc, emb,
           out_lp, out_y,
           hid_v, wq_v, wk_v, wv_v, kb, vb, wo_v, wg_v, wu_v, wd_v, emb_v,
           p1, q1, h1, a1, act, s2, r2, xs, gs, zb, g_all, h_v, fz, fy, fx, fc,
           lsem, kvsem, ssem, c_rs, x_rs, r_rs, z_rs, a_rs, b_rs, d_rs, fz_rs, fy_rs, fx_rs):
    D = hid.shape[1]
    N = hid.shape[0]
    HD = wk.shape[1]
    FH = wg_v.shape[1]
    L = D // 128
    LP = s2.shape[0] // (2 * NT)
    R = 2 * NT
    DH = D // 2
    CTX = kc.shape[1]
    t = lax.axis_index('t')
    v = lax.axis_index('v')
    c = lax.rem(v, 2)
    y = lax.rem(v // 2, NY)
    z = v // (2 * NY)
    me_r = 2 * t + c

    def dev(tt, zz, yy, cc):
        return {'t': tt, 'v': (zz * NY + yy) * 2 + cc}

    partner = dev(t, z, y, 1 - c)
    x_peers = [(lax.rem(t + k, NT), dev(lax.rem(t + k, NT), z, y, c)) for k in range(1, NT)]
    y_peers = [(lax.rem(y + k, NY), dev(t, z, lax.rem(y + k, NY), c)) for k in range(1, NY)]
    z_peers = [(lax.rem(z + k, NZ), dev(t, lax.rem(z + k, NZ), y, c)) for k in range(1, NZ)]
    r_peers = []
    for k in range(1, R):
        rr = lax.rem(me_r + k, R)
        r_peers.append((rr, dev(rr // 2, z, y, lax.rem(rr, 2))))
    own_a = jnp.where(c == 0, y, t)
    own_b = jnp.where(c == 0, t, y)
    a_peers = []
    b_peers = []
    for k in range(1, NT):
        a_peers.append((lax.rem(own_a + k, NT), dev(lax.rem(t + k * c, NT), z, lax.rem(y + k * (1 - c), NY), c)))
        b_peers.append((lax.rem(own_b + k, NT), dev(lax.rem(t + k * (1 - c), NT), z, lax.rem(y + k * c, NY), c)))

    def token_of(r):
        rx, rc = r // 2, r % 2
        if rc == 0:
            return (rx * NT + y) * NZ + z
        return ((NT + y) * NT + rx) * NZ + z

    tokens = [token_of(r) for r in range(R)]
    chd = pl.ds(pl.multiple_of(c * HD, HD), HD)
    cfh = pl.ds(pl.multiple_of(c * FH, 128), FH)
    loads = {}

    def load(name, src, dst, sem):
        loads[name] = pltpu.make_async_copy(src, dst, sem)
        loads[name].start()

    load('hid', hid, hid_v, lsem.at[0])
    load('wq', wq.at[:, chd], wq_v, lsem.at[1])
    load('wk', wk, wk_v, lsem.at[2])
    load('wv', wv, wv_v, lsem.at[3])
    for r in range(R):
        load('k%d' % r, kc.at[tokens[r]], kb.at[r], kvsem.at[r])
    for r in range(R):
        load('v%d' % r, vc.at[tokens[r]], vb.at[r], kvsem.at[R + r])
    load('wo', wo.at[chd], wo_v, lsem.at[4])
    load('wg', wg.at[:, cfh], wg_v, lsem.at[5])
    load('wu', wu.at[:, cfh], wu_v, lsem.at[6])
    load('wd', wd.at[cfh], wd_v, lsem.at[7])
    load('emb', emb, emb_v, lsem.at[8])

    barrier = pltpu.get_barrier_semaphore()
    greeted = [partner] + [d for _, d in x_peers + y_peers + z_peers]
    for k in range(1, NT):
        greeted.append(dev(lax.rem(t + k, NT), z, y, 1 - c))
    for d in greeted:
        pl.semaphore_signal(barrier, inc=1, device_id=d, device_id_type=MESH)

    sent = []

    def send(src, dst, recv_sem, device):
        copy = pltpu.make_async_remote_copy(
            src_ref=src, dst_ref=dst, send_sem=ssem.at[len(sent)], recv_sem=recv_sem,
            device_id=device, device_id_type=MESH)
        copy.start()
        sent.append(copy)

    def arrived(ref, recv_sem):
        pltpu.make_async_remote_copy(
            src_ref=ref, dst_ref=ref, send_sem=ssem.at[0], recv_sem=recv_sem,
            device_id=partner, device_id_type=MESH).wait_recv()

    s2[...] = jnp.zeros_like(s2)
    xs[...] = jnp.zeros_like(xs)
    gs[...] = jnp.zeros_like(gs)
    g_mo_row = g_mo[...].astype(F32).reshape(1, D)
    for l in range(L):
        gs[pl.ds(l, 1), :] = g_mo_row[:, 128 * l:128 * (l + 1)]

    rr = lax.broadcasted_iota(jnp.int32, (R, 1), 0)
    rx, rc = lax.shift_right_logical(rr, 1), jnp.bitwise_and(rr, 1)
    token_col = jnp.where(rc == 0, (rx * NT + y) * NZ + z, ((NT + y) * NT + rx) * NZ + z)
    pick = jnp.where(lax.broadcasted_iota(jnp.int32, (R, N), 1) == token_col, 1.0, 0.0).astype(BF16)
    pos = jnp.zeros((R, 1), jnp.int32)
    for r in range(R):
        pos = jnp.where(rr == r, seq[tokens[r]], pos)
    angles = pos.astype(F32) * inv_freq[...]
    cos_t = jnp.cos(angles)
    sin_t = jnp.sin(angles)

    def rotary(values):
        low, high = values[:, :HD // 2], values[:, HD // 2:]
        return jnp.concatenate([low * cos_t - high * sin_t, high * cos_t + low * sin_t], axis=-1).astype(BF16)

    loads['hid'].wait()
    x = dot(pick, hid_v[...])
    normed = rms(x, g_ap[...].astype(F32).reshape(1, D)).astype(BF16)
    loads['wq'].wait()
    q_rot = rotary(dot(normed, wq_v[...]))
    loads['wk'].wait()
    k_rot = rotary(dot(normed, wk_v[...]))
    loads['wv'].wait()
    v_new = dot(normed, wv_v[...]).astype(BF16)
    scale = HD ** -0.5
    s_cache = jnp.zeros((R, CTX), F32)
    for r in range(R):
        loads['k%d' % r].wait()
        s_cache = jnp.where(rr == r, dot_nt(q_rot, kb[r]), s_cache)
    s_new = jnp.sum(q_rot.astype(F32) * k_rot.astype(F32), axis=-1, keepdims=True) * scale
    s_cache = ATTN_CAP * jnp.tanh(s_cache * scale / ATTN_CAP)
    s_new = ATTN_CAP * jnp.tanh(s_new / ATTN_CAP)
    valid = lax.broadcasted_iota(jnp.int32, (R, CTX), 1) < pos
    s_cache = jnp.where(valid, s_cache, -1e30)
    row_max = jnp.maximum(jnp.max(s_cache, axis=-1, keepdims=True), s_new)
    p_cache = jnp.exp(s_cache - row_max)
    p_new = jnp.exp(s_new - row_max)
    denominator = jnp.sum(p_cache, axis=-1, keepdims=True) + p_new
    p_bf = p_cache.astype(BF16)
    weighted = jnp.zeros((R, HD), F32)
    for r in range(R):
        loads['v%d' % r].wait()
        weighted = jnp.where(rr == r, dot(p_bf, vb[r]), weighted)
    weighted = weighted + p_new.astype(BF16).astype(F32) * v_new.astype(F32)
    attn_vec = (weighted / denominator).astype(BF16)
    loads['wo'].wait()
    attn_part = dot(attn_vec, wo_v[...])
    p1[0] = attn_part[:, :DH]
    p1[1] = attn_part[:, DH:]

    pl.semaphore_wait(barrier, len(greeted))
    send(p1.at[1 - c], q1, c_rs.at[0], partner)
    arrived(q1, c_rs.at[0])
    h1[t] = p1[c] + q1[...]
    for _, d in x_peers:
        send(h1.at[t], h1.at[t], x_rs.at[t], d)
    for k, _ in x_peers:
        arrived(h1.at[k], x_rs.at[k])
    half = h1[0]
    for k in range(1, NT):
        half = half + h1[k]
    a1[c] = half
    send(a1.at[c], a1.at[c], c_rs.at[1], partner)
    arrived(a1.at[1 - c], c_rs.at[1])
    attn_out = jnp.concatenate([a1[0], a1[1]], axis=-1)
    mid = (x + rms(attn_out, g_ao[...].astype(F32).reshape(1, D))).astype(BF16).astype(F32)
    for l in range(L):
        xs[pl.ds(l, R, stride=LP), :] = mid[:, 128 * l:128 * (l + 1)]
    mlp_in = rms(mid, g_mp[...].astype(F32).reshape(1, D)).astype(BF16)

    loads['wg'].wait()
    loads['wu'].wait()
    width = 384 if FH % 384 == 0 else 128
    for j in range(FH // width):
        cols = pl.ds(j * width, width)
        gate = dot(mlp_in, wg_v[:, cols])
        up = dot(mlp_in, wu_v[:, cols])
        act[:, cols] = (jax.nn.gelu(gate, approximate=True) * up).astype(BF16)
    loads['wd'].wait()
    width = 768 if D % 768 == 0 else 128
    for j in range(D // width):
        part = dot(act[...], wd_v[:, pl.ds(j * width, width)])
        for i in range(width // 128):
            s2[pl.ds(j * (width // 128) + i, R, stride=LP), :] = part[:, 128 * i:128 * (i + 1)]

    def slot(k):
        return pl.ds(pl.multiple_of(k * LP, 8), LP)

    for k, d in r_peers:
        send(s2.at[slot(k)], r2.at[slot(me_r)], r_rs.at[me_r], d)
    r2[slot(me_r), :] = s2[slot(me_r), :]
    for k, _ in r_peers:
        arrived(r2.at[slot(k)], r_rs.at[k])
    row = r2[pl.ds(0, LP), :]
    for k in range(1, R):
        row = row + r2[pl.ds(k * LP, LP), :]
    mean_sq = jnp.sum(jnp.sum(row * row, axis=0, keepdims=True), axis=1, keepdims=True) * (1.0 / D)
    row = row * lax.rsqrt(mean_sq + NORM_EPS) * (1.0 + gs[...])
    zb[slot(z), :] = (xs[slot(me_r), :] + row).astype(BF16).astype(F32)

    for _, d in z_peers:
        send(zb.at[slot(z)], zb.at[slot(z)], z_rs.at[z], d)
    for k, _ in z_peers:
        arrived(zb.at[slot(k)], z_rs.at[k])
    first = c * NT + own_b
    mine = first * NT + own_a
    for l in range(L):
        g_all[mine, :, 128 * l:128 * (l + 1)] = zb[pl.ds(l, NZ, stride=LP), :]
    for _, d in a_peers:
        send(g_all.at[mine], g_all.at[mine], a_rs.at[own_a], d)
    for k, _ in a_peers:
        arrived(g_all.at[first * NT + k], a_rs.at[k])
    whole = pl.ds(first * NT, NT)
    for _, d in b_peers:
        send(g_all.at[whole], g_all.at[whole], b_rs.at[own_b], d)
    send(g_all.at[whole], g_all.at[whole], d_rs.at[own_b], partner)
    for k, _ in b_peers:
        piece = pl.ds((c * NT + k) * NT, NT)
        arrived(g_all.at[piece], b_rs.at[k])
        send(g_all.at[piece], g_all.at[piece], d_rs.at[k], partner)

    g_fi_row = g_fi[...].astype(F32).reshape(1, D)
    step = min(16 // NZ, NT * NT)
    width = step * NZ

    def final_norm(core):
        def body(i, carry):
            blk = core * (NT * NT) + i * step
            ys = g_all[pl.ds(blk, step)].reshape(width, D)
            rows = pl.ds(pl.multiple_of(blk * NZ, width), width)
            out_y[rows, :] = ys.astype(BF16)
            h_v[rows, :] = rms(ys, g_fi_row).astype(BF16)
            return carry
        lax.fori_loop(0, NT * NT // step, body, 0)

    final_norm(c)
    for k in range(NT):
        arrived(g_all.at[pl.ds(((1 - c) * NT + k) * NT, NT)], d_rs.at[k])
    final_norm(1 - c)

    loads['emb'].wait()
    VL = emb.shape[0]
    rows_at = 0
    total = jnp.zeros((1, N), F32)
    hit = jnp.zeros((1, N), F32)
    target = tgt[...].reshape(1, N) - (v * NT + t) * VL
    while rows_at < VL:
        size = min(256, VL - rows_at)
        logits = dot_nt(emb_v[pl.ds(rows_at, size), :], h_v[...])
        capped = FINAL_CAP * jnp.tanh(logits / FINAL_CAP)
        total = total + jnp.sum(jnp.exp(capped), axis=0, keepdims=True)
        ids = rows_at + lax.broadcasted_iota(jnp.int32, (size, N), 0)
        hit = hit + jnp.sum(jnp.where(ids == target, capped, 0.0), axis=0, keepdims=True)
        rows_at += size
    stats = jnp.concatenate([total, hit], axis=0)

    for buf, sems, me, peers, count in (
        (fz, fz_rs, z, z_peers, NZ), (fy, fy_rs, y, y_peers, NY), (fx, fx_rs, t, x_peers, NT),
        (fc, None, c, [(1 - c, partner)], 2)):
        buf[me] = stats
        for k, d in peers:
            send(buf.at[me], buf.at[me], c_rs.at[2] if sems is None else sems.at[me], d)
        for k, d in peers:
            arrived(buf.at[k], c_rs.at[2] if sems is None else sems.at[k])
        stats = buf[0]
        for k in range(1, count):
            stats = stats + buf[k]
    out_lp[...] = stats[1:2, :] - jnp.log(stats[0:1, :])
    for copy in sent:
        copy.wait_send()


def solution(mesh):
    NT = mesh.shape['t']
    V = mesh.shape['v']
    NY = NT
    NZ = V // (2 * NY)
    in_specs = (P(), P(), P(), P(), P(None, 't'), P(None, 't'), P(None, 't'), P('t', None), P(), P(), P(None, 't'), P(None, 't'), P('t', None), P(), P(), P(None, None, 't', None), P(None, None, 't', None), P(('v', 't'), None))

    def local_step(hidden_in, seq_lens, target, g_attn_pre, w_q, w_k, w_v, w_o, g_attn_post, g_mlp_pre, w_gate, w_up, w_down, g_mlp_post, g_final, k_cache, v_cache, embed_table):
        N, D = hidden_in.shape
        CTX, _, HD = k_cache.shape[1:]
        FH = w_gate.shape[1] // 2
        VL = embed_table.shape[0]
        R = 2 * NT
        LP = (D // 128 + 7) // 8 * 8
        inv_freq = (ROPE_BASE ** (-2.0 * np.arange(HD // 2, dtype=np.float32) / HD)).astype(np.float32).reshape(1, HD // 2)
        any_spec = pl.BlockSpec(memory_space=pl.ANY)
        vmem = pl.BlockSpec(memory_space=pltpu.VMEM)
        smem = pl.BlockSpec(memory_space=pltpu.SMEM)
        sends = 3 + 3 * (NT - 1) + (R - 1) + (NZ - 1) + NT + (NZ - 1) + (NY - 1) + (NT - 1) + 1
        dma = pltpu.SemaphoreType.DMA
        lp, hidden_out = pl.pallas_call(
            functools.partial(kernel, NT, NY, NZ),
            name='decode_step',
            out_shape=(jax.ShapeDtypeStruct((1, N), F32), jax.ShapeDtypeStruct((N, D), BF16)),
            in_specs=[smem, any_spec] + [vmem] * 7 + [any_spec] * 10,
            out_specs=(vmem, vmem),
            scratch_shapes=[
                pltpu.VMEM((N, D), BF16), pltpu.VMEM((D, HD), BF16), pltpu.VMEM((D, HD), BF16), pltpu.VMEM((D, HD), BF16),
                pltpu.VMEM((R, CTX, HD), BF16), pltpu.VMEM((R, CTX, HD), BF16), pltpu.VMEM((HD, D), BF16),
                pltpu.VMEM((D, FH), BF16), pltpu.VMEM((D, FH), BF16), pltpu.VMEM((FH, D), BF16), pltpu.VMEM((VL, D), BF16),
                pltpu.VMEM((2, R, D // 2), F32), pltpu.VMEM((R, D // 2), F32), pltpu.VMEM((NT, R, D // 2), F32),
                pltpu.VMEM((2, R, D // 2), F32), pltpu.VMEM((R, FH), BF16),
                pltpu.VMEM((R * LP, 128), F32), pltpu.VMEM((R * LP, 128), F32), pltpu.VMEM((R * LP, 128), F32),
                pltpu.VMEM((LP, 128), F32), pltpu.VMEM((NZ * LP, 128), F32),
                pltpu.VMEM((2 * NT * NT, NZ, D), F32), pltpu.VMEM((N, D), BF16),
                pltpu.VMEM((NZ, 2, N), F32), pltpu.VMEM((NY, 2, N), F32), pltpu.VMEM((NT, 2, N), F32), pltpu.VMEM((2, 2, N), F32),
                dma((9,)), dma((2 * R,)), dma((sends,)), dma((3,)), dma((NT,)), dma((R,)), dma((NZ,)), dma((NT,)), dma((NT,)),
                dma((NT,)), dma((NZ,)), dma((NY,)), dma((NT,)),
            ],
            compiler_params=pltpu.CompilerParams(
                collective_id=0, has_side_effects=True, vmem_limit_bytes=60 * 1024 * 1024),
        )(seq_lens, hidden_in, target, inv_freq, g_attn_pre, g_attn_post, g_mlp_pre, g_mlp_post, g_final,
          w_q, w_k, w_v, w_o, w_gate, w_up, w_down,
          k_cache.reshape(N, CTX, HD), v_cache.reshape(N, CTX, HD), embed_table)
        return lp.reshape(N), hidden_out

    return jax.shard_map(local_step, mesh=mesh, in_specs=in_specs, out_specs=(P(), P()), check_vma=False)
```

time: 332 us -> 70.6 us (0.21)
  waiting for transfers between devices: 138 us -> 0 us
  blocking collectives: 74 us -> 0 us
  matrix products: 70.6 us -> 0 us
  Pallas kernels: 0 us -> 66.2 us
  other arithmetic: 20.5 us -> 0 us
  between operations: 14.2 us -> 0.65 us
  local copies, waits for them, and re-layouts: 13.3 us -> 3.58 us
    psum x2 -> x0, waiting for transfers between devices: 138 us -> none  [the longest x1 70.8 us: local_step(): attn_out = lax.psum(attn_part, 't')]
    all_gather x1 -> x0, blocking collectives: 74 us -> none  [local_step(): lax.all_gather(jnp.stack([local_max, local_sum, local_tgt]), ('v', 't'))]
    dot_general x9 -> x0, matrix products: 70.6 us -> none  [the longest x1 16.3 us: attention(): jnp.einsum('nkgd,ntkd->nkgt', q_rot, k_cache, preferred_element_type=jnp....]
    pallas_call x0 -> x1, Pallas kernels: none -> 66.2 us  [local_step(): pl.pallas_call(functools.partial(kernel, NT, NY, NZ), name='decode_step',...]
    reduce_sum x9 -> x0, other arithmetic: 10.3 us -> none  [the longest x5 7.02 us: rms_norm(): jnp.mean(x_f32 * x_f32, axis=-1, keepdims=True) + NORM_EPS]
  transfers between devices with their start and end apart: 2 -> 0, of which waited for: 2 -> 0; matrix products, arithmetic and copies ran while one was open for 0% -> 0% of each run, Pallas kernels for 0% -> 0%
where the time goes in v1:
time: 70.6 us; the launch traced here: 70.4 us
  Pallas kernels  66.2 us (94%)
  local copies, waits for them, and re-layouts  3.58 us (5%)
    pallas_call x1, Pallas kernels, local_step(): pl.pallas_call(functools.partial(kernel, NT, NY, NZ), name='decode_step',...  66.2 us
    unnamed x2, local copies, waits for them, and re-layouts  3.58 us

profile of v1, /device:TPU:1, one launch (start us, length us, event | category | flops | bytes accessed | tf_op | source)
XLA Modules:
  0.0 70.4 jit_solution(13076960523481825328)
XLA Ops:
  0.6 66.2 %decode_step.1 = (f32[1,256]{1,0:T(1,128)}, bf16[256,2304]{1,0:T(8,128)(2,1)}) custom-call(s32[256]{0:T(256)} %seq.1, bf16[256,2304]{1,0:T(8,128)(2,1)} %hid.1, s32[256]{0:T(256)} %tgt.1, f32[1,128]{1,0:T(1,128)} %constant.2.clone.inv_freq, bf16[2304]{0:T(1024)(128)(2,1)} %g_ap.1, bf16[2304]{0:T(1024)(128)(2,1)} %g_ao.1, bf16[2304]{0:T(1024)(128)(2,1)} %g_mp.1, ...), custom_call_target="tpu_custom_call" | custom-call | tf_op jit(solution)/shard_map/decode_step/pallas_call | solution.py:322
  66.9 1.2 %copy.23 = f32[256]{0:T(256)} copy(f32[256]{0:T(256)} %bitcast.5) | data formatting | bytes 2048
  68.1 2.4 %copy.24 = bf16[256,2304]{1,0:T(8,128)(2,1)} copy(bf16[256,2304]{1,0:T(8,128)(2,1)} %get-tuple-element.9) | data formatting | bytes 2359296

commit v2 on v1

v2 whole, which is shorter than its diff:
```python
import functools

import jax
import jax.numpy as jnp
import numpy as np
from jax import lax
from jax.experimental import pallas as pl
from jax.experimental.pallas import tpu as pltpu
from jax.sharding import PartitionSpec as P

ATTN_CAP = 50.0
FINAL_CAP = 30.0
NORM_EPS = 1e-6
ROPE_BASE = 10000.0
MESH = pl.DeviceIdType.MESH
F32 = jnp.float32
BF16 = jnp.bfloat16
VMEM_LIMIT = 60 * 1024 * 1024


def dot(a, b):
    return jnp.dot(a, b, preferred_element_type=F32)


def dot_nt(a, b):
    return lax.dot_general(a, b, (((1,), (1,)), ((), ())), preferred_element_type=F32)


def rms(values, gain):
    mean_sq = jnp.mean(values * values, axis=-1, keepdims=True)
    return values * lax.rsqrt(mean_sq + NORM_EPS) * (1.0 + gain)


def kernel(NT, NY, NZ, seq_h, hid, tgt_h, freq_h, ap_h, ao_h, mp_h, mo_h, fi_h, wq, wk, wv, wo, wg, wu, wd, kc, vc, emb,
           out_lp, out_y,
           seq, tgt, inv_freq, g_ap, g_ao, g_mp, g_mo, g_fi, y_v, hid_v, wq_v, wk_v, wv_v, kb, vb, wo_v, wg_v, wu_v, wd_v, emb_v,
           act, s1, s2, r1, r2, m1, xs, gs, gt, h_v, fz, fx,
           lsem, ssem, r_rs, z_rs, a_rs, b_rs, d_rs, f_rs):
    N, D = hid.shape
    HD = wk.shape[1]
    FH = wg_v.shape[1]
    CTX = kc.shape[1]
    VL = emb.shape[0]
    L = D // 128
    R = 2 * NT
    LP = s1.shape[0] // R
    PZ = NZ // 2
    t = lax.axis_index('t')
    v = lax.axis_index('v')
    c = lax.rem(v, 2)
    y = lax.rem(v // 2, NY)
    z = v // (2 * NY)
    me_r = 2 * t + c

    def dev(tt, zz, yy, cc):
        return {'t': tt, 'v': (zz * NY + yy) * 2 + cc}

    partner = dev(t, z, y, 1 - c)
    near_first = sorted(range(1, NZ), key=lambda k: min(k, NZ - k))
    ring = [k for k in (1, NT - 1, 2) if 0 < k < NT]
    ring = sorted(set(ring), key=ring.index)
    z_peers = [(lax.rem(z + k, NZ), dev(t, lax.rem(z + k, NZ), y, c)) for k in near_first]
    r_peers = []
    for k in range(1, R):
        rr = lax.rem(me_r + k, R)
        r_peers.append((rr, dev(rr // 2, z, y, lax.rem(rr, 2))))
    own_a = jnp.where(c == 0, y, t)
    own_b = jnp.where(c == 0, t, y)
    a_peers = []
    b_peers = []
    for k in ring:
        a_peers.append((lax.rem(own_a + k, NT), dev(lax.rem(t + k * c, NT), z, lax.rem(y + k * (1 - c), NY), c)))
        b_peers.append((lax.rem(own_b + k, NT), dev(lax.rem(t + k * (1 - c), NT), z, lax.rem(y + k * c, NY), c)))
    zc_peers = []
    for dz in [0] + near_first:
        for dc in (0, 1):
            if dz or dc:
                zz, cc = lax.rem(z + dz, NZ), (c if dc == 0 else 1 - c)
                zc_peers.append((zz * 2 + cc, dev(t, zz, y, cc)))
    xy_peers = []
    for dx in range(NT):
        for dy in range(NY):
            if dx or dy:
                xx, yy = lax.rem(t + dx, NT), lax.rem(y + dy, NY)
                xy_peers.append((xx * NY + yy, dev(xx, z, yy, c)))

    def token_of(r):
        rx, rc = r // 2, r % 2
        if rc == 0:
            return (rx * NT + y) * NZ + z
        return ((NT + y) * NT + rx) * NZ + z

    tokens = [token_of(r) for r in range(R)]
    chd = pl.ds(pl.multiple_of(c * HD, HD), HD)
    cfh = pl.ds(pl.multiple_of(c * FH, 128), FH)
    loads = {}

    def load(name, src, dst, sem):
        loads[name] = pltpu.make_async_copy(src, dst, sem)
        loads[name].start()

    load('seq', seq_h, seq, lsem.at[11])
    load('freq', freq_h, inv_freq, lsem.at[12])
    load('ap', ap_h, g_ap, lsem.at[13])
    load('hid', hid, hid_v, lsem.at[0])
    load('wq', wq.at[:, chd], wq_v, lsem.at[1])
    load('wk', wk, wk_v, lsem.at[2])
    load('wv', wv, wv_v, lsem.at[3])
    for r in range(R):
        load('k%d' % r, kc.at[tokens[r]], kb.at[r], lsem.at[9])
    for r in range(R):
        load('v%d' % r, vc.at[tokens[r]], vb.at[r], lsem.at[10])
    for i, (src, dst) in enumerate(((tgt_h, tgt), (ao_h, g_ao), (mp_h, g_mp), (mo_h, g_mo), (fi_h, g_fi))):
        load('small%d' % i, src, dst, lsem.at[14 + i])
    load('wo', wo.at[chd], wo_v, lsem.at[4])
    load('wg', wg.at[:, cfh], wg_v, lsem.at[5])
    load('wu', wu.at[:, cfh], wu_v, lsem.at[6])
    load('wd', wd.at[cfh], wd_v, lsem.at[7])
    load('emb', emb, emb_v, lsem.at[8])

    barrier = pltpu.get_barrier_semaphore()
    greeted = [d for _, d in zc_peers + xy_peers]
    for k in range(1, NT):
        greeted.append(dev(lax.rem(t + k, NT), z, y, 1 - c))
    for d in greeted:
        pl.semaphore_signal(barrier, inc=1, device_id=d, device_id_type=MESH)

    def send(src, dst, lane, recv_sem, device):
        pltpu.make_async_remote_copy(
            src_ref=src, dst_ref=dst, send_sem=ssem.at[lane], recv_sem=recv_sem,
            device_id=device, device_id_type=MESH).start()

    def all_sent(ref, lane):
        pltpu.make_async_remote_copy(
            src_ref=ref, dst_ref=ref, send_sem=ssem.at[lane], recv_sem=z_rs.at[0],
            device_id=partner, device_id_type=MESH).wait_send()

    def arrived(ref, recv_sem):
        pltpu.make_async_remote_copy(
            src_ref=ref, dst_ref=ref, send_sem=ssem.at[0], recv_sem=recv_sem,
            device_id=partner, device_id_type=MESH).wait_recv()

    for buf in (s1, s2, xs, gs):
        buf[...] = jnp.zeros_like(buf)
    def slot(k):
        return pl.ds(pl.multiple_of(k * LP, 8), LP)

    def to_rows(buf, values, at):
        for i in range(values.shape[1] // 128):
            buf[pl.ds(at + i, R, stride=LP), :] = values[:, 128 * i:128 * (i + 1)]

    others = pl.ds(0, (R - 1) * LP)

    def reduce_rows(src, dst, lane):
        for k, d in r_peers:
            send(src.at[slot(k)], dst.at[slot(me_r)], lane, r_rs.at[lane], d)
        dst[slot(me_r), :] = src[slot(me_r), :]
        arrived(dst.at[others], r_rs.at[lane])
        row = dst[pl.ds(0, LP), :]
        for k in range(1, R):
            row = row + dst[pl.ds(k * LP, LP), :]
        return row

    def rms_row(row, i):
        mean_sq = jnp.sum(jnp.sum(row * row, axis=0, keepdims=True), axis=1, keepdims=True) * (1.0 / D)
        return row * lax.rsqrt(mean_sq + NORM_EPS) * (1.0 + gs[pl.ds(i * LP, LP), :])

    rr = lax.broadcasted_iota(jnp.int32, (R, 1), 0)
    rx, rc = lax.shift_right_logical(rr, 1), jnp.bitwise_and(rr, 1)
    token_col = jnp.where(rc == 0, (rx * NT + y) * NZ + z, ((NT + y) * NT + rx) * NZ + z)
    pick = jnp.where(lax.broadcasted_iota(jnp.int32, (R, N), 1) == token_col, 1.0, 0.0).astype(BF16)
    loads['seq'].wait()
    loads['freq'].wait()
    loads['ap'].wait()
    pos = jnp.zeros((R, 1), jnp.int32)
    for r in range(R):
        pos = jnp.where(rr == r, seq[tokens[r]], pos)
    angles = pos.astype(F32) * inv_freq[...]
    cos_t = jnp.cos(angles)
    sin_t = jnp.sin(angles)

    def rotary(values):
        low, high = values[:, :HD // 2], values[:, HD // 2:]
        return jnp.concatenate([low * cos_t - high * sin_t, high * cos_t + low * sin_t], axis=-1).astype(BF16)

    loads['hid'].wait()
    x = dot(pick, hid_v[...])
    normed = rms(x, g_ap[...].astype(F32).reshape(1, D)).astype(BF16)
    to_rows(xs, x, 0)
    for name in ('wq', 'wk', 'wv'):
        loads[name].wait()
    q_rot = rotary(dot(normed, wq_v[...]))
    k_rot = rotary(dot(normed, wk_v[...]))
    v_new = dot(normed, wv_v[...]).astype(BF16)
    scale = HD ** -0.5
    pltpu.make_async_copy(kb, kb, lsem.at[9]).wait()
    scores = [dot_nt(q_rot, kb[r]) for r in range(R)]
    s_cache = scores[0]
    for r in range(1, R):
        s_cache = jnp.where(rr == r, scores[r], s_cache)
    s_new = jnp.sum(q_rot.astype(F32) * k_rot.astype(F32), axis=-1, keepdims=True) * scale
    s_cache = ATTN_CAP * jnp.tanh(s_cache * scale / ATTN_CAP)
    s_new = ATTN_CAP * jnp.tanh(s_new / ATTN_CAP)
    valid = lax.broadcasted_iota(jnp.int32, (R, CTX), 1) < pos
    s_cache = jnp.where(valid, s_cache, -1e30)
    row_max = jnp.maximum(jnp.max(s_cache, axis=-1, keepdims=True), s_new)
    p_cache = jnp.exp(s_cache - row_max)
    p_new = jnp.exp(s_new - row_max)
    denominator = jnp.sum(p_cache, axis=-1, keepdims=True) + p_new
    p_bf = p_cache.astype(BF16)
    pltpu.make_async_copy(vb, vb, lsem.at[10]).wait()
    parts = [dot(p_bf, vb[r]) for r in range(R)]
    weighted = parts[0]
    for r in range(1, R):
        weighted = jnp.where(rr == r, parts[r], weighted)
    weighted = weighted + p_new.astype(BF16).astype(F32) * v_new.astype(F32)
    attn_vec = (weighted / denominator).astype(BF16)
    loads['wo'].wait()
    to_rows(s1, dot(attn_vec, wo_v[...]), 0)
    for i in range(5):
        loads['small%d' % i].wait()
    for i, gain in enumerate((g_ao, g_mo)):
        gain_row = gain[...].astype(F32).reshape(1, D)
        for l in range(L):
            gs[pl.ds(i * LP + l, 1), :] = gain_row[:, 128 * l:128 * (l + 1)]

    pl.semaphore_wait(barrier, len(greeted))
    row = reduce_rows(s1, r1, 0)
    mid_row = (xs[slot(me_r), :] + rms_row(row, 0)).astype(BF16).astype(F32)
    m1[slot(me_r), :] = mid_row
    for _, d in r_peers:
        send(m1.at[slot(me_r)], m1.at[slot(me_r)], 1, r_rs.at[1], d)
    arrived(m1.at[others], r_rs.at[1])
    mid = jnp.concatenate([m1[pl.ds(l, R, stride=LP), :] for l in range(L)], axis=-1)
    mlp_in = rms(mid, g_mp[...].astype(F32).reshape(1, D)).astype(BF16)

    loads['wg'].wait()
    loads['wu'].wait()
    width = 384 if FH % 384 == 0 else 128
    for j in range(FH // width):
        cols = pl.ds(j * width, width)
        gate = dot(mlp_in, wg_v[:, cols])
        up = dot(mlp_in, wu_v[:, cols])
        act[:, cols] = (jax.nn.gelu(gate, approximate=True) * up).astype(BF16)
    loads['wd'].wait()
    width = 768 if D % 768 == 0 else 128
    for j in range(D // width):
        to_rows(s2, dot(act[...], wd_v[:, pl.ds(j * width, width)]), j * (width // 128))
    row = reduce_rows(s2, r2, 2)
    y_row = (m1[slot(me_r), :] + rms_row(row, 1)).astype(BF16).astype(F32)

    def pair(core, b, a, q):
        return pl.ds((((core * NT + b) * NT + a) * NZ + 2 * q) * L, 2 * L)

    def single(zz):
        return pl.ds((((c * NT + own_b) * NT + own_a) * NZ + zz) * L, L)

    me_at = (((c * NT + own_b) * NT + own_a) * NZ + z) * L
    for l in range(L):
        gt[me_at + l] = y_row[l:l + 1, :]
    my_q = z // 2
    for _, d in z_peers:
        send(gt.at[single(z)], gt.at[single(z)], 3, z_rs.at[my_q], d)

    def rows_of(count):
        return gt.at[pl.ds(0, count * L)]

    def to_b_and_core(a, q, late):
        here = gt.at[pair(c, own_b, a, q)]
        for _, d in b_peers:
            send(here, here, 5, b_rs.at[(own_b * PZ + q) * 2 + late], d)
        send(here, here, 6, d_rs.at[own_b], partner)

    def own_pair(dq):
        q = lax.rem(my_q + dq, PZ)
        arrived(rows_of(1 if dq == 0 else 2), z_rs.at[q])
        here = gt.at[pair(c, own_b, own_a, q)]
        for _, d in a_peers:
            send(here, here, 4, a_rs.at[q], d)
        to_b_and_core(own_a, q, 0)

    def first_axis(dq):
        q = lax.rem(my_q + dq, PZ)
        arrived(rows_of(2 * (NT - 1)), a_rs.at[q])
        for a, _ in a_peers:
            to_b_and_core(a, q, 1)

    if PZ == 4:
        own_pair(0)
        own_pair(1)
        own_pair(3)
        first_axis(0)
        own_pair(2)
        first_axis(1)
        first_axis(3)
        first_axis(2)
    else:
        for dq in range(PZ):
            own_pair(dq)
        for dq in range(PZ):
            first_axis(dq)
    order = [0, 1, 3, 2] if PZ == 4 else list(range(PZ))

    g_fi_row = 1.0 + g_fi[...].astype(F32).reshape(1, D)
    unit = 16 if NT * NZ % 16 == 0 else NT * NZ

    def final_norm(core, b):
        def body(i, carry):
            first = (core * NT + b) * (NT * NZ) + i * unit
            tiles = []
            for l in range(L):
                tiles.append(jnp.concatenate(
                    [gt[pl.ds((first + j) * L + l, NZ, stride=L), 0, :] for j in range(0, unit, NZ)], axis=0))
            square = tiles[0] * tiles[0]
            for l in range(1, L):
                square = square + tiles[l] * tiles[l]
            inv = lax.rsqrt(jnp.sum(square, axis=-1, keepdims=True) * (1.0 / D) + NORM_EPS)
            rows = pl.ds(pl.multiple_of(first, unit), unit)
            for l in range(L):
                cols = slice(128 * l, 128 * (l + 1))
                y_v[rows, cols] = tiles[l].astype(BF16)
                h_v[rows, cols] = (tiles[l] * inv * g_fi_row[:, cols]).astype(BF16)
            return carry
        lax.fori_loop(0, NT * NZ // unit, body, 0)

    final_norm(c, own_b)
    for i, (b, _) in enumerate(b_peers):
        for late, lanes in ((0, [own_a]), (1, [a for a, _ in a_peers])):
            for dq in order:
                q = lax.rem(my_q + dq, PZ)
                arrived(rows_of(2 * len(lanes)), b_rs.at[(b * PZ + q) * 2 + late])
                for a in lanes:
                    piece = gt.at[pair(c, b, a, q)]
                    send(piece, piece, 6, d_rs.at[b], partner)
        if i + 1 < len(b_peers):
            final_norm(c, b)
    final_norm(c, b_peers[-1][0])
    for k in [0] + ring:
        b = lax.rem(own_a + k, NT)
        arrived(rows_of(NT * NZ), d_rs.at[b])
        final_norm(1 - c, b)

    load('y', y_v, out_y, lsem.at[19])

    loads['emb'].wait()
    rows_at = 0
    total = jnp.zeros((1, N), F32)
    hit = jnp.zeros((1, N), F32)
    target = tgt[...].reshape(1, N) - (v * NT + t) * VL
    while rows_at < VL:
        size = min(256, VL - rows_at)
        logits = dot_nt(emb_v[pl.ds(rows_at, size), :], h_v[...])
        capped = FINAL_CAP * jnp.tanh(logits * (1.0 / FINAL_CAP))
        total = total + jnp.sum(jnp.exp(capped), axis=0, keepdims=True)
        ids = rows_at + lax.broadcasted_iota(jnp.int32, (size, N), 0)
        hit = hit + jnp.sum(jnp.where(ids == target, capped, 0.0), axis=0, keepdims=True)
        rows_at += size
    stats = jnp.concatenate([total, hit], axis=0)

    for i, (buf, me, peers) in enumerate(((fz, z * 2 + c, zc_peers), (fx, t * NY + y, xy_peers))):
        buf[me] = stats
        for _, d in peers:
            send(buf.at[me], buf.at[me], 7 + i, f_rs.at[i], d)
        arrived(buf.at[pl.ds(0, len(peers))], f_rs.at[i])
        stats = buf[0]
        for k in range(1, buf.shape[0]):
            stats = stats + buf[k]
    out_lp[...] = stats[1:2, :] - jnp.log(stats[0:1, :])
    loads['y'].wait()
    for lane, ref in enumerate((
            s1.at[others], m1.at[others], s2.at[others], rows_of(NZ - 1), rows_of(PZ * 2 * (NT - 1)),
            rows_of(NT * PZ * 2 * (NT - 1)), rows_of(NT * NT * NZ), fz.at[pl.ds(0, len(zc_peers))],
            fx.at[pl.ds(0, len(xy_peers))])):
        all_sent(ref, lane)


def hand_on(parts, lp_in, y_in, lp_out, y_out, lp_v, y_v, sems):
    rows = y_v.shape[1]
    first = pltpu.make_async_copy(lp_in, lp_v, sems.at[0])
    first.start()
    into = [pltpu.make_async_copy(y_in.at[pl.ds(i * rows, rows)], y_v.at[i], sems.at[1 + i]) for i in range(parts)]
    for copy in into:
        copy.start()
    first.wait()
    out = [pltpu.make_async_copy(lp_v, lp_out, sems.at[1 + parts])]
    out[0].start()
    for i in range(parts):
        into[i].wait()
        out.append(pltpu.make_async_copy(y_v.at[i], y_out.at[pl.ds(i * rows, rows)], sems.at[2 + parts + i]))
        out[-1].start()
    for copy in out:
        copy.wait()


def solution(mesh):
    NT = mesh.shape['t']
    V = mesh.shape['v']
    NY = NT
    NZ = V // (2 * NY)
    in_specs = (P(), P(), P(), P(), P(None, 't'), P(None, 't'), P(None, 't'), P('t', None), P(), P(), P(None, 't'), P(None, 't'), P('t', None), P(), P(), P(None, None, 't', None), P(None, None, 't', None), P(('v', 't'), None))

    def local_step(hidden_in, seq_lens, target, g_attn_pre, w_q, w_k, w_v, w_o, g_attn_post, g_mlp_pre, w_gate, w_up, w_down, g_mlp_post, g_final, k_cache, v_cache, embed_table):
        N, D = hidden_in.shape
        CTX, _, HD = k_cache.shape[1:]
        FH = w_gate.shape[1] // 2
        VL = embed_table.shape[0]
        R = 2 * NT
        LP = (D // 128 + 7) // 8 * 8
        inv_freq = (ROPE_BASE ** (-2.0 * np.arange(HD // 2, dtype=np.float32) / HD)).astype(np.float32).reshape(1, HD // 2)
        vmem = pl.BlockSpec(memory_space=pltpu.VMEM)
        PZ = NZ // 2
        dma = pltpu.SemaphoreType.DMA
        rows = pltpu.VMEM((R * LP, 128), F32)
        lp, hidden_out = pl.pallas_call(
            functools.partial(kernel, NT, NY, NZ),
            name='decode_step',
            out_shape=(jax.ShapeDtypeStruct((1, N), F32), jax.ShapeDtypeStruct((N, D), BF16)),
            in_specs=[pl.BlockSpec(memory_space=pltpu.HBM)] * 19,
            out_specs=(vmem, pl.BlockSpec(memory_space=pltpu.HBM)),
            scratch_shapes=[
                pltpu.SMEM((N,), jnp.int32), pltpu.VMEM((N,), jnp.int32), pltpu.VMEM((1, HD // 2), F32)]
            + [pltpu.VMEM((D,), BF16)] * 5 + [
                pltpu.VMEM((N, D), BF16), pltpu.VMEM((N, D), BF16), pltpu.VMEM((D, HD), BF16), pltpu.VMEM((D, HD), BF16), pltpu.VMEM((D, HD), BF16),
                pltpu.VMEM((R, CTX, HD), BF16), pltpu.VMEM((R, CTX, HD), BF16), pltpu.VMEM((HD, D), BF16),
                pltpu.VMEM((D, FH), BF16), pltpu.VMEM((D, FH), BF16), pltpu.VMEM((FH, D), BF16), pltpu.VMEM((VL, D), BF16),
                pltpu.VMEM((R, FH), BF16), rows, rows, rows, rows, rows, rows, pltpu.VMEM((2 * LP, 128), F32),
                pltpu.VMEM((N * (D // 128), 1, 128), F32), pltpu.VMEM((N, D), BF16),
                pltpu.VMEM((2 * NZ, 2, N), F32), pltpu.VMEM((NT * NY, 2, N), F32),
                dma((20,)), dma((9,)), dma((3,)), dma((PZ,)), dma((PZ,)), dma((NT * PZ * 2,)), dma((NT,)), dma((2,)),
            ],
            compiler_params=pltpu.CompilerParams(
                collective_id=0, has_side_effects=True, vmem_limit_bytes=VMEM_LIMIT),
        )(seq_lens, hidden_in, target, inv_freq, g_attn_pre, g_attn_post, g_mlp_pre, g_mlp_post, g_final,
          w_q, w_k, w_v, w_o, w_gate, w_up, w_down,
          k_cache.reshape(N, CTX, HD), v_cache.reshape(N, CTX, HD), embed_table)
        parts = 4 if N % 64 == 0 else 1
        hbm = pl.BlockSpec(memory_space=pltpu.HBM)
        lp, hidden_out = pl.pallas_call(
            functools.partial(hand_on, parts),
            name='hand_on',
            out_shape=(jax.ShapeDtypeStruct((1, N), F32), jax.ShapeDtypeStruct((N, D), BF16)),
            in_specs=[hbm, hbm],
            out_specs=(hbm, hbm),
            scratch_shapes=[pltpu.VMEM((1, N), F32), pltpu.VMEM((parts, N // parts, D), BF16), dma((2 + 2 * parts,))],
            compiler_params=pltpu.CompilerParams(vmem_limit_bytes=VMEM_LIMIT),
        )(lp, hidden_out)
        return lp.reshape(N), hidden_out

    return jax.shard_map(local_step, mesh=mesh, in_specs=in_specs, out_specs=(P(), P()), check_vma=False)
```

time: 70.6 us -> 58.1 us (0.82)
  Pallas kernels: 66.2 us -> 57.3 us
  local copies, waits for them, and re-layouts: 3.58 us -> 0 us
    pallas_call x1, Pallas kernels: 66.2 us -> 55.3 us  [local_step(): pl.pallas_call(functools.partial(kernel, NT, NY, NZ), name='decode_step',...]
    unnamed x2 -> x0, local copies, waits for them, and re-layouts: 3.58 us -> none
    pallas_call x0 -> x1, Pallas kernels: none -> 2.06 us  [local_step(): pl.pallas_call(functools.partial(hand_on, parts), name='hand_on', out_sha...]
where the time goes in v2:
time: 58.1 us; the launch traced here: 58 us
  Pallas kernels  57.3 us (99%)
  between operations  0.65 us (1%)
    pallas_call x1, Pallas kernels, local_step(): pl.pallas_call(functools.partial(kernel, NT, NY, NZ), name='decode_step',...  55.3 us
    pallas_call x1, Pallas kernels, local_step(): pl.pallas_call(functools.partial(hand_on, parts), name='hand_on', out_sha...  2.06 us

profile of v2, /device:TPU:1, one launch (start us, length us, event | category | flops | bytes accessed | tf_op | source)
XLA Modules:
  0.0 58.0 jit_solution(1434174839481822541)
XLA Ops:
  0.6 55.3 %decode_step.1 = (f32[1,256]{1,0:T(1,128)}, bf16[256,2304]{1,0:T(8,128)(2,1)}) custom-call(s32[256]{0:T(256)} %seq_h.1, bf16[256,2304]{1,0:T(8,128)(2,1)} %hid.1, s32[256]{0:T(256)} %tgt_h.1, f32[1,128]{1,0:T(1,128)} %constant.2.clone.freq_h, bf16[2304]{0:T(1024)(128)(2,1)} %ap_h.1, bf16[2304]{0:T(1024)(128)(2,1)} %ao_h.1, bf16[2304]{0:T(1024)(128)(2,1)} %mp_h.1, ...), custom_call_target="tpu_custom_call" | custom-call | tf_op jit(solution)/shard_map/decode_step/pallas_call | solution.py:414
  55.9 2.1 %hand_on.1 = (f32[1,256]{1,0:T(1,128)}, bf16[256,2304]{1,0:T(8,128)(2,1)}) custom-call(f32[1,256]{1,0:T(1,128)} %get-tuple-element.6.lp_in, bf16[256,2304]{1,0:T(8,128)(2,1)} %get-tuple-element.7.y_in), custom_call_target="tpu_custom_call" | custom-call | tf_op jit(solution)/shard_map/hand_on/pallas_call | solution.py:438

commit v3 on v2

--- a/solution.py
+++ b/solution.py
@@ -59,9 +59,10 @@
     near_first = sorted(range(1, NZ), key=lambda k: min(k, NZ - k))
     ring = [k for k in (1, NT - 1, 2) if 0 < k < NT]
     ring = sorted(set(ring), key=ring.index)
-    z_peers = [(lax.rem(z + k, NZ), dev(t, lax.rem(z + k, NZ), y, c)) for k in near_first]
+    z_order = [k for k in near_first if k in (1, NZ - 1)] + [k for k in near_first[::-1] if k not in (1, NZ - 1)]
+    z_peers = [(lax.rem(z + k, NZ), dev(t, lax.rem(z + k, NZ), y, c)) for k in z_order]
     r_peers = []
-    for k in range(1, R):
+    for k in sorted(range(1, R), key=lambda k: -min(k // 2, NT - k // 2)):
         rr = lax.rem(me_r + k, R)
         r_peers.append((rr, dev(rr // 2, z, y, lax.rem(rr, 2))))
     own_a = jnp.where(c == 0, y, t)
@@ -72,17 +73,16 @@
         a_peers.append((lax.rem(own_a + k, NT), dev(lax.rem(t + k * c, NT), z, lax.rem(y + k * (1 - c), NY), c)))
         b_peers.append((lax.rem(own_b + k, NT), dev(lax.rem(t + k * (1 - c), NT), z, lax.rem(y + k * c, NY), c)))
     zc_peers = []
-    for dz in [0] + near_first:
+    for dz in near_first[::-1] + [0]:
         for dc in (0, 1):
             if dz or dc:
                 zz, cc = lax.rem(z + dz, NZ), (c if dc == 0 else 1 - c)
                 zc_peers.append((zz * 2 + cc, dev(t, zz, y, cc)))
     xy_peers = []
-    for dx in range(NT):
-        for dy in range(NY):
-            if dx or dy:
-                xx, yy = lax.rem(t + dx, NT), lax.rem(y + dy, NY)
-                xy_peers.append((xx * NY + yy, dev(xx, z, yy, c)))
+    steps = [(dx, dy) for dx in range(NT) for dy in range(NY) if dx or dy]
+    for dx, dy in sorted(steps, key=lambda s: -min(s[0], NT - s[0]) - min(s[1], NY - s[1])):
+        xx, yy = lax.rem(t + dx, NT), lax.rem(y + dy, NY)
+        xy_peers.append((xx * NY + yy, dev(xx, z, yy, c)))
 
     def token_of(r):
         rx, rc = r // 2, r % 2
@@ -113,10 +113,6 @@
     for i, (src, dst) in enumerate(((tgt_h, tgt), (ao_h, g_ao), (mp_h, g_mp), (mo_h, g_mo), (fi_h, g_fi))):
         load('small%d' % i, src, dst, lsem.at[14 + i])
     load('wo', wo.at[chd], wo_v, lsem.at[4])
-    load('wg', wg.at[:, cfh], wg_v, lsem.at[5])
-    load('wu', wu.at[:, cfh], wu_v, lsem.at[6])
-    load('wd', wd.at[cfh], wd_v, lsem.at[7])
-    load('emb', emb, emb_v, lsem.at[8])
 
     barrier = pltpu.get_barrier_semaphore()
     greeted = [d for _, d in zc_peers + xy_peers]
@@ -194,6 +190,10 @@
     v_new = dot(normed, wv_v[...]).astype(BF16)
     scale = HD ** -0.5
     pltpu.make_async_copy(kb, kb, lsem.at[9]).wait()
+    load('wg', wg.at[:, cfh], wg_v, lsem.at[5])
+    load('wu', wu.at[:, cfh], wu_v, lsem.at[6])
+    load('wd', wd.at[cfh], wd_v, lsem.at[7])
+    load('emb', emb, emb_v, lsem.at[8])
     scores = [dot_nt(q_rot, kb[r]) for r in range(R)]
     s_cache = scores[0]
     for r in range(1, R):
@@ -321,24 +321,33 @@
                 y_v[rows, cols] = tiles[l].astype(BF16)
                 h_v[rows, cols] = (tiles[l] * inv * g_fi_row[:, cols]).astype(BF16)
             return carry
-        lax.fori_loop(0, NT * NZ // unit, body, 0)
-
-    final_norm(c, own_b)
-    for i, (b, _) in enumerate(b_peers):
-        for late, lanes in ((0, [own_a]), (1, [a for a, _ in a_peers])):
-            for dq in order:
-                q = lax.rem(my_q + dq, PZ)
-                arrived(rows_of(2 * len(lanes)), b_rs.at[(b * PZ + q) * 2 + late])
-                for a in lanes:
-                    piece = gt.at[pair(c, b, a, q)]
-                    send(piece, piece, 6, d_rs.at[b], partner)
-        if i + 1 < len(b_peers):
-            final_norm(c, b)
-    final_norm(c, b_peers[-1][0])
-    for k in [0] + ring:
+        lax.fori_loop(0, NT * NZ // unit, body, 0, unroll=True)
+
+    def second_axis(b, dq, late):
+        q = lax.rem(my_q + dq, PZ)
+        lanes = [a for a, _ in a_peers] if late else [own_a]
+        arrived(rows_of(2 * len(lanes)), b_rs.at[(b * PZ + q) * 2 + late])
+        for a in lanes:
+            piece = gt.at[pair(c, b, a, q)]
+            send(piece, piece, 6, d_rs.at[b], partner)
+
+    def other_core(k):
         b = lax.rem(own_a + k, NT)
         arrived(rows_of(NT * NZ), d_rs.at[b])
         final_norm(1 - c, b)
+
+    final_norm(c, own_b)
+    for dq in order:
+        for b, _ in b_peers:
+            second_axis(b, dq, 0)
+    other_core(0)
+    for dq in order:
+        for b, _ in b_peers:
+            second_axis(b, dq, 1)
+    for b, _ in b_peers:
+        final_norm(c, b)
+    for k in ring:
+        other_core(k)
 
     load('y', y_v, out_y, lsem.at[19])
 

time: 58.1 us -> 56.5 us (0.972)
  Pallas kernels: 57.3 us -> 55.8 us
    pallas_call x1, Pallas kernels: 55.3 us -> 53.7 us  [local_step(): pl.pallas_call(functools.partial(kernel, NT, NY, NZ), name='decode_step',...]
where the time goes in v3:
time: 56.5 us; the launch traced here: 56.4 us
  Pallas kernels  55.8 us (99%)
  between operations  0.65 us (1%)
    pallas_call x1, Pallas kernels, local_step(): pl.pallas_call(functools.partial(kernel, NT, NY, NZ), name='decode_step',...  53.7 us
    pallas_call x1, Pallas kernels, local_step(): pl.pallas_call(functools.partial(hand_on, parts), name='hand_on', out_sha...  2.06 us

profile of v3, /device:TPU:1, one launch (start us, length us, event | category | flops | bytes accessed | tf_op | source)
XLA Modules:
  0.0 56.4 jit_solution(15535868319384344180)
XLA Ops:
  0.6 53.7 %decode_step.1 = (f32[1,256]{1,0:T(1,128)}, bf16[256,2304]{1,0:T(8,128)(2,1)}) custom-call(s32[256]{0:T(256)} %seq_h.1, bf16[256,2304]{1,0:T(8,128)(2,1)} %hid.1, s32[256]{0:T(256)} %tgt_h.1, f32[1,128]{1,0:T(1,128)} %constant.2.clone.freq_h, bf16[2304]{0:T(1024)(128)(2,1)} %ap_h.1, bf16[2304]{0:T(1024)(128)(2,1)} %ao_h.1, bf16[2304]{0:T(1024)(128)(2,1)} %mp_h.1, ...), custom_call_target="tpu_custom_call" | custom-call | tf_op jit(solution)/shard_map/decode_step/pallas_call | solution.py:423
  54.4 2.1 %hand_on.1 = (f32[1,256]{1,0:T(1,128)}, bf16[256,2304]{1,0:T(8,128)(2,1)}) custom-call(f32[1,256]{1,0:T(1,128)} %get-tuple-element.6.lp_in, bf16[256,2304]{1,0:T(8,128)(2,1)} %get-tuple-element.7.y_in), custom_call_target="tpu_custom_call" | custom-call | tf_op jit(solution)/shard_map/hand_on/pallas_call | solution.py:447

commit v4 on v3

--- a/solution.py
+++ b/solution.py
@@ -141,15 +141,24 @@
     def slot(k):
         return pl.ds(pl.multiple_of(k * LP, 8), LP)
 
+    per = L // (LP // 8)
+
+    def at_row(l):
+        return l // per * 8 + l % per
+
     def to_rows(buf, values, at):
         for i in range(values.shape[1] // 128):
-            buf[pl.ds(at + i, R, stride=LP), :] = values[:, 128 * i:128 * (i + 1)]
+            buf[pl.ds(at_row(at + i), R, stride=LP), :] = values[:, 128 * i:128 * (i + 1)]
 
     others = pl.ds(0, (R - 1) * LP)
 
+    def send_group(src, dst, lane, group):
+        def part(k):
+            return pl.ds(pl.multiple_of(k * LP + 8 * group, 8), 8)
+        for k, d in r_peers:
+            send(src.at[part(k)], dst.at[part(me_r)], lane, r_rs.at[lane], d)
+
     def reduce_rows(src, dst, lane):
-        for k, d in r_peers:
-            send(src.at[slot(k)], dst.at[slot(me_r)], lane, r_rs.at[lane], d)
         dst[slot(me_r), :] = src[slot(me_r), :]
         arrived(dst.at[others], r_rs.at[lane])
         row = dst[pl.ds(0, LP), :]
@@ -222,16 +231,18 @@
     for i, gain in enumerate((g_ao, g_mo)):
         gain_row = gain[...].astype(F32).reshape(1, D)
         for l in range(L):
-            gs[pl.ds(i * LP + l, 1), :] = gain_row[:, 128 * l:128 * (l + 1)]
+            gs[pl.ds(i * LP + at_row(l), 1), :] = gain_row[:, 128 * l:128 * (l + 1)]
 
     pl.semaphore_wait(barrier, len(greeted))
+    for k, d in r_peers:
+        send(s1.at[slot(k)], r1.at[slot(me_r)], 0, r_rs.at[0], d)
     row = reduce_rows(s1, r1, 0)
     mid_row = (xs[slot(me_r), :] + rms_row(row, 0)).astype(BF16).astype(F32)
     m1[slot(me_r), :] = mid_row
     for _, d in r_peers:
         send(m1.at[slot(me_r)], m1.at[slot(me_r)], 1, r_rs.at[1], d)
     arrived(m1.at[others], r_rs.at[1])
-    mid = jnp.concatenate([m1[pl.ds(l, R, stride=LP), :] for l in range(L)], axis=-1)
+    mid = jnp.concatenate([m1[pl.ds(at_row(l), R, stride=LP), :] for l in range(L)], axis=-1)
     mlp_in = rms(mid, g_mp[...].astype(F32).reshape(1, D)).astype(BF16)
 
     loads['wg'].wait()
@@ -243,9 +254,9 @@
         up = dot(mlp_in, wu_v[:, cols])
         act[:, cols] = (jax.nn.gelu(gate, approximate=True) * up).astype(BF16)
     loads['wd'].wait()
-    width = 768 if D % 768 == 0 else 128
-    for j in range(D // width):
-        to_rows(s2, dot(act[...], wd_v[:, pl.ds(j * width, width)]), j * (width // 128))
+    for j in range(LP // 8):
+        to_rows(s2, dot(act[...], wd_v[:, pl.ds(j * per * 128, per * 128)]), j * per)
+        send_group(s2, r2, 2, j)
     row = reduce_rows(s2, r2, 2)
     y_row = (m1[slot(me_r), :] + rms_row(row, 1)).astype(BF16).astype(F32)
 
@@ -257,7 +268,7 @@
 
     me_at = (((c * NT + own_b) * NT + own_a) * NZ + z) * L
     for l in range(L):
-        gt[me_at + l] = y_row[l:l + 1, :]
+        gt[me_at + l] = y_row[at_row(l):at_row(l) + 1, :]
     my_q = z // 2
     for _, d in z_peers:
         send(gt.at[single(z)], gt.at[single(z)], 3, z_rs.at[my_q], d)
@@ -414,7 +425,7 @@
         FH = w_gate.shape[1] // 2
         VL = embed_table.shape[0]
         R = 2 * NT
-        LP = (D // 128 + 7) // 8 * 8
+        LP = 24 if D % 384 == 0 else (D // 128 + 7) // 8 * 8
         inv_freq = (ROPE_BASE ** (-2.0 * np.arange(HD // 2, dtype=np.float32) / HD)).astype(np.float32).reshape(1, HD // 2)
         vmem = pl.BlockSpec(memory_space=pltpu.VMEM)
         PZ = NZ // 2

time: 56.5 us -> 56.7 us (level)
  no operation moved by 1% of the time
where the time goes in v4:
time: 56.7 us; the launch traced here: 56.6 us
  Pallas kernels  56 us (99%)
  between operations  0.65 us (1%)
    pallas_call x1, Pallas kernels, local_step(): pl.pallas_call(functools.partial(kernel, NT, NY, NZ), name='decode_step',...  53.9 us
    pallas_call x1, Pallas kernels, local_step(): pl.pallas_call(functools.partial(hand_on, parts), name='hand_on', out_sha...  2.06 us

profile of v4, /device:TPU:1, one launch (start us, length us, event | category | flops | bytes accessed | tf_op | source)
XLA Modules:
  0.0 56.6 jit_solution(14374132282314029217)
XLA Ops:
  0.6 53.9 %decode_step.1 = (f32[1,256]{1,0:T(1,128)}, bf16[256,2304]{1,0:T(8,128)(2,1)}) custom-call(s32[256]{0:T(256)} %seq_h.1, bf16[256,2304]{1,0:T(8,128)(2,1)} %hid.1, s32[256]{0:T(256)} %tgt_h.1, f32[1,128]{1,0:T(1,128)} %constant.2.clone.freq_h, bf16[2304]{0:T(1024)(128)(2,1)} %ap_h.1, bf16[2304]{0:T(1024)(128)(2,1)} %ao_h.1, bf16[2304]{0:T(1024)(128)(2,1)} %mp_h.1, ...), custom_call_target="tpu_custom_call" | custom-call | tf_op jit(solution)/shard_map/decode_step/pallas_call | solution.py:434
  54.6 2.1 %hand_on.1 = (f32[1,256]{1,0:T(1,128)}, bf16[256,2304]{1,0:T(8,128)(2,1)}) custom-call(f32[1,256]{1,0:T(1,128)} %get-tuple-element.6.lp_in, bf16[256,2304]{1,0:T(8,128)(2,1)} %get-tuple-element.7.y_in), custom_call_target="tpu_custom_call" | custom-call | tf_op jit(solution)/shard_map/hand_on/pallas_call | solution.py:458
